TPU v7x, 128 devices: a whole 4x4x4 slice. The times are simulated.
128 devices in a mesh: rep: 16 (over y, x_hi, core), fsdp: 8 (over x_lo, z).
Axes of the slice: x: 4 (x_hi: 2, x_lo: 2; x = x_hi * 2 + x_lo), y: 4, z: 4, core: 2. Of those that a mesh axis runs over, the one named last changes fastest.
Arguments:
- replica_inner_weight: bfloat16 [16, 1024, 16384], P('rep', 'fsdp'), may hold values from -30 to 30
- outer_weights: float32 [1024, 16384], P('fsdp'), may hold values from -6 to 6
- momentum: float32 [1024, 16384], P('fsdp', 'rep'), may hold values from -4 to 4
- exponents: int32 [16, 1024, 128], P('rep', 'fsdp'), may hold values from 0 to 2
- levels: int32 [16], replicated, may hold values from -60 to 60, as said below
Outputs:
- inner_next: bfloat16 [16, 1024, 16384], P('rep', 'fsdp')
- momentum_next: float32 [1024, 16384], P('fsdp', 'rep')
- outer_next: float32 [1024, 16384], P('fsdp', 'rep')
Inputs may be any that keep to these rules, and one draw needn't show every extreme that they name: `levels`: 16 distinct values, half of them negative and half positive, ascending.
All inputs are finite; a program needn't handle non-finite values. Where the computation divides by a largest or mean magnitude, that divisor is 1e-20 or more.
Results may differ from a plain program's by a relative error of at most 0.0085.
Values may be sent and summed in bfloat16 or wider, within the bound.
No kernel may reach another device: no remote copies, remote signals or barrier semaphores. Data moves between devices by JAX's collectives and lax.ppermute only.
A program may use at most 128 MiB of HBM per device.

v0:
```python
import jax
import jax.numpy as jnp
from jax import lax
from jax.sharding import Mesh
from jax.sharding import PartitionSpec as P

NLEV = 16
REP = ("rep_0", "rep_1", "rep_2")
FSDP = ("fsdp_0", "fsdp_1")
REP_FSDP = ("rep_0", "rep_1", "rep_2", "fsdp_0", "fsdp_1")


softness_factor = 0.02
clip_rms = 0.1
outer_rate = 0.7
outer_mu = 0.9
mix_rate = 0.5


def by_axis(array, axes):
    for axis in axes:
        array = lax.psum(array, axis)
    return array


def encode_grad(pseudo_grad, exponents, levels):
    quantize_grid_points = levels.astype(jnp.float32) / jnp.max(jnp.abs(levels)).astype(jnp.float32)
    block_scale = jnp.exp2(exponents.astype(jnp.float32))[..., None]
    row_count = pseudo_grad.shape[0]
    rescaled_gradient = pseudo_grad.reshape(row_count, exponents.shape[-1], -1) / block_scale
    closest_grid_level = (rescaled_gradient - quantize_grid_points[0]) ** 2
    for grid_level_index in range(1, NLEV):
        closest_grid_level = jnp.minimum(
            closest_grid_level, (rescaled_gradient - quantize_grid_points[grid_level_index]) ** 2
        )
    weighted = jnp.zeros_like(rescaled_gradient)
    weights_sum = jnp.zeros_like(rescaled_gradient)
    for grid_level_index in range(NLEV):
        current_weight = jnp.exp(
            -(
                (rescaled_gradient - quantize_grid_points[grid_level_index]) ** 2
                - closest_grid_level
            )
            / softness_factor
        )
        weighted = weighted + current_weight * quantize_grid_points[grid_level_index]
        weights_sum = weights_sum + current_weight
    coded = block_scale * weighted / weights_sum
    return coded.reshape(row_count, -1).astype(jnp.bfloat16)


def clip_factor(squares, entries):
    return jnp.minimum(
        jnp.float32(1.0), clip_rms / jnp.sqrt(squares / jnp.float32(entries) + 1e-06)
    )


def per_device(replica_inner_weight, outer_weights, momentum, exponents, levels):
    replicas = lax.axis_size(REP)
    row_count, columns = outer_weights.shape
    entries = row_count * lax.axis_size(FSDP) * columns
    width = momentum.shape[1]
    start = lax.axis_index(REP) * width
    coded = encode_grad(
        outer_weights - replica_inner_weight[0].astype(jnp.float32), exponents[0], levels
    )
    share = lax.psum_scatter(coded, REP, scatter_dimension=1, tiled=True).astype(jnp.float32)
    mean_grad = share / jnp.float32(replicas)
    squares = by_axis(jnp.sum(mean_grad * mean_grad), REP_FSDP)
    grad = clip_factor(squares, entries) * mean_grad
    momentum_next = outer_mu * momentum + grad
    outer_piece = lax.dynamic_slice_in_dim(outer_weights, start, width, 1)
    outer_next = outer_piece - outer_rate * (grad + outer_mu * momentum_next)
    outer_half = lax.all_gather(outer_next.astype(jnp.bfloat16), REP, axis=1, tiled=True)
    mixed = mix_rate * outer_half.astype(jnp.float32) + (1.0 - mix_rate) * replica_inner_weight[
        0
    ].astype(jnp.float32)
    inner_next = mixed.astype(jnp.bfloat16)[None]
    return (inner_next, momentum_next, outer_next)


def solution(mesh):
    torus = Mesh(
        mesh.devices.reshape(4, 2, 2, 2, 4), ("rep_0", "rep_1", "rep_2", "fsdp_0", "fsdp_1")
    )
    placed = (P(REP, FSDP, None), P(FSDP, None), P(FSDP, REP), P(REP, FSDP, None), P())
    return jax.shard_map(
        per_device,
        mesh=torus,
        in_specs=placed,
        out_specs=(P(REP, FSDP, None), P(FSDP, REP), P(FSDP, REP)),
        check_vma=False,
    )
```

profile of v0, /device:TPU:1, one launch (start us, length us, event | category | flops | bytes accessed | tf_op | source)
XLA Modules:
  0.0 264.6 jit_solution(7247658938995126674)
XLA Ops:
  7.2 0.0 reduce-scatter.2.cloned.1.call-start
  7.2 1.3 abs_reduce_fusion
  9.2 0.0 copy-start
  9.2 0.8 convert_divide_fusion
  10.0 0.7 fusion.15
  10.7 0.9 exponential_bitcast_fusion
  11.6 2.3 mul.130
  13.9 0.0 copy-done
  13.9 0.0 copy-start.1
  13.9 60.4 %fusion.4 = bf16[128,16384]{1,0:T(8,128)(2,1)} fusion(f32[128,16384]{1,0:T(8,128)} %param.6, f32[16,8,128,128]{3,2,1,0:T(8,128)S(1)} %bitcast.34, bf16[1,128,16384]{2,1,0:T(8,128)(2,1)S(1)} %copy-done, f32[]{:T(128)} %bitcast.17, f32[]{:T(128)} %bitcast.16, f32[]{:T(128)} %bitcast.15, f32[]{:T(128)} %bitcast.14, f32[]{:T(128)} %bitcast.13, f32[]{:T(128)} %bitcast.12, ...), kind=kLoop, calls=%fused_computation.7 | loop fusion | flops 308281344 | bytes 25165888 | tf_op jit(solution)/shard_map/convert_element_type | solution.py:49
  74.3 0.0 reduce-scatter.2.cloned.1.call-update
  74.3 0.0 all-gather.2.cloned.1.call-start
  74.4 82.5 %reduce-scatter.2.cloned.1.call-done = bf16[128,1024]{1,0:T(8,128)(2,1)} async-done(((bf16[128,16384]{1,0:T(8,128)(2,1)}), bf16[128,1024]{1,0:T(8,128)(2,1)}) %reduce-scatter.2.cloned.1.call-update) | async-done | bytes 262160 | tf_op jit(solution)/shard_map/reduce_scatter | solution.py:67
  156.9 1.7 fusion.11
  158.5 8.7 %psum.35 = f32[]{:T(128)} all-reduce(f32[]{:T(128)} %fusion.11), channel_id=1, replica_groups=mesh['rep_0'=4,'rep_1'=2,'rep_2'=2,'fsdp_0'=2,'fsdp_1'=4] {'rep_0'}, use_global_device_ids=true, to_apply=%region_3.0 | all-reduce | flops 1 | bytes 8 | tf_op jit(solution)/shard_map/psum | solution.py:22
  167.3 5.9 %psum.36 = f32[]{:T(128)} all-reduce(f32[]{:T(128)} %psum.35), channel_id=1, replica_groups=mesh['rep_0'=4,'rep_1'=2,'rep_2'=2,'fsdp_0'=2,'fsdp_1'=4] {'rep_1'}, use_global_device_ids=true, to_apply=%region_4.0 | all-reduce | flops 1 | bytes 8 | tf_op jit(solution)/shard_map/psum | solution.py:22
  173.2 7.9 %psum.37 = f32[]{:T(128)} all-reduce(f32[]{:T(128)} %psum.36), channel_id=1, replica_groups=mesh['rep_0'=4,'rep_1'=2,'rep_2'=2,'fsdp_0'=2,'fsdp_1'=4] {'rep_2'}, use_global_device_ids=true, to_apply=%region_5.0 | all-reduce | flops 1 | bytes 8 | tf_op jit(solution)/shard_map/psum | solution.py:22
  181.1 4.4 %psum.38 = f32[]{:T(128)} all-reduce(f32[]{:T(128)} %psum.37), channel_id=1, replica_groups=mesh['rep_0'=4,'rep_1'=2,'rep_2'=2,'fsdp_0'=2,'fsdp_1'=4] {'fsdp_0'}, use_global_device_ids=true, to_apply=%region_6.0 | all-reduce | flops 1 | bytes 8 | tf_op jit(solution)/shard_map/psum | solution.py:22
  185.5 9.3 %psum.39 = f32[]{:T(128)} all-reduce(f32[]{:T(128)} %psum.38), channel_id=1, replica_groups=mesh['rep_0'=4,'rep_1'=2,'rep_2'=2,'fsdp_0'=2,'fsdp_1'=4] {'fsdp_1'}, use_global_device_ids=true, to_apply=%region_7.0 | all-reduce | flops 1 | bytes 8 | tf_op jit(solution)/shard_map/psum | solution.py:22
  195.4 0.0 copy-done.1
  195.4 2.3 fusion.12
  197.8 0.0 all-gather.2.cloned.1.call-update
  197.8 53.3 %all-gather.2.cloned.1.call-done = bf16[128,16384]{1,0:T(8,128)(2,1)} async-done(((bf16[128,1024]{1,0:T(8,128)(2,1)}), bf16[128,16384]{1,0:T(8,128)(2,1)}) %all-gather.2.cloned.1.call-update) | async-done | bytes 4194320 | tf_op jit(solution)/shard_map/all_gather | solution.py:74
  251.1 6.7 %fusion.5 = bf16[1,128,16384]{2,1,0:T(8,128)(2,1)} fusion(bf16[128,16384]{1,0:T(8,128)(2,1)} %all-gather.2.cloned.1.call-done, bf16[1,128,16384]{2,1,0:T(8,128)(2,1)} %param.5), kind=kLoop, calls=%fused_computation.8 | loop fusion | flops 10485760 | bytes 12582912 | tf_op jit(solution)/shard_map/broadcast_in_dim | solution.py:78
Async XLA Ops:
  7.2 149.7 %reduce-scatter.2.cloned.1.call-start = ((), (), s32[]{:S(2)}) async-start(), calls=%async_computation.1 | async-start | bytes 4456448 | tf_op jit(solution)/shard_map/reduce_scatter | solution.py:67
  9.2 4.7 %copy-start = (bf16[1,128,16384]{2,1,0:T(8,128)(2,1)S(1)}, bf16[1,128,16384]{2,1,0:T(8,128)(2,1)}, u32[]{:S(2)}) copy-start(bf16[1,128,16384]{2,1,0:T(8,128)(2,1)} %param.5) | copy-start | bytes 12582916
  13.9 181.5 %copy-start.1 = (f32[128,1024]{1,0:T(8,128)S(1)}, f32[128,1024]{1,0:T(8,128)}, u32[]{:S(2)}) copy-start(f32[128,1024]{1,0:T(8,128)} %param.7) | copy-start | bytes 1572868
  74.3 176.8 %all-gather.2.cloned.1.call-start = ((), (), s32[]{:S(2)}) async-start(), calls=%async_computation.2 | async-start | bytes 4456448 | tf_op jit(solution)/shard_map/all_gather | solution.py:74
Sparse Core Ops, SparseCore 0:
  74.4 82.3 reduce-scatter.1
  197.9 53.0 all-gather.1
where the time goes:
time: 265 us
  waiting for transfers between devices  136 us (51%)
  other arithmetic  74.1 us (28%)
  blocking collectives  36.2 us (14%)
  between operations  15.4 us (6%)
  local copies, waits for them, and re-layouts  3.03 us (1%)
    reduce_scatter x1, waiting for transfers between devices, per_device(): lax.psum_scatter(coded, REP, scatter_dimension=1, tiled=True)  82.5 us
    convert_element_type x1, other arithmetic, encode_grad(): return coded.reshape(row_count, -1).astype(jnp.bfloat16)  60.4 us
    all_gather x1, waiting for transfers between devices, per_device(): lax.all_gather(outer_next.astype(jnp.bfloat16), REP, axis=1, tiled=True)  53.3 us
    psum x5, blocking collectives, by_axis(): array = lax.psum(array, axis)  36.2 us
    broadcast_in_dim x1, other arithmetic, per_device(): inner_next = mixed.astype(jnp.bfloat16)[None]  6.7 us
  transfers between devices with their start and end apart: 2, of which 2 were waited for; matrix products, arithmetic and copies ran while one was open for 0% of the time, Pallas kernels for 0%

commit v1 on v0

v1 whole, which is shorter than its diff:
```python
import math

import jax
import jax.numpy as jnp
from jax import lax
from jax.experimental import pallas as pl
from jax.experimental.pallas import tpu as pltpu
from jax.sharding import Mesh
from jax.sharding import PartitionSpec as P

NLEV = 16
LANES = 128
REP = ("rep_0", "rep_1", "rep_2")
CHIPS = ("rep_0", "rep_1")
CORE = "rep_2"
FSDP = ("fsdp_0", "fsdp_1")

softness_factor = 0.02
clip_rms = 0.1
outer_rate = 0.7
outer_mu = 0.9
mix_rate = 0.5

STRETCH = math.sqrt(1.0 / (softness_factor * math.log(2.0)))
WIDTHS = (512, 512)
GROUP = 256
TILE = 64


def prepare(levels):
    def body(lev, grid_ref, sum_ref):
        top = jnp.abs(lev[0])
        for k in range(1, NLEV):
            top = jnp.maximum(top, jnp.abs(lev[k]))
        top = jnp.full((8, LANES), top, jnp.int32).astype(jnp.float32)
        row = lax.broadcasted_iota(jnp.int32, (LANES, 2 * LANES), 0)
        col = lax.broadcasted_iota(jnp.int32, (LANES, 2 * LANES), 1)
        for k in range(NLEV):
            lk = jnp.full((8, LANES), lev[k], jnp.int32).astype(jnp.float32)
            grid_ref[k] = lk / top * STRETCH
            level = jnp.full((LANES, 2 * LANES), lev[k], jnp.int32)
            one = jnp.where(row == col, 1, jnp.where(row + LANES == col, level, 0))
            sum_ref[k * LANES:(k + 1) * LANES, :] = one.astype(jnp.float32).astype(jnp.bfloat16)
        grid_ref[NLEV] = 1.0 / top

    return pl.pallas_call(
        body,
        in_specs=[pl.BlockSpec(memory_space=pltpu.SMEM)],
        out_shape=(
            jax.ShapeDtypeStruct((NLEV + 1, 8, LANES), jnp.float32),
            jax.ShapeDtypeStruct((NLEV * LANES, 2 * LANES), jnp.bfloat16),
        ),
        name="prepare",
    )(levels)


def encode(where, grid, summing, outer, inner, exponents, width, received=None):
    rows = outer.shape[0]
    owners = 8
    per_step = max(1, 1024 // width)
    steps = owners // per_step
    blocks = width // LANES
    group_blocks = GROUP // rows
    groups = [(a, g) for a in range(per_step) for g in range(blocks // group_blocks)]

    def body(*refs):
        idx, grid_ref, sum_ref, exp_ref = refs[:4]
        outer_refs = refs[4:4 + per_step]
        inner_refs = refs[4 + per_step:4 + 2 * per_step]
        rest = refs[4 + 2 * per_step:]
        recv_ref = rest[0] if received is not None else None
        out_ref = rest[-1]
        step = pl.program_id(0)
        lanes = lax.broadcasted_iota(jnp.int32, (TILE, LANES), 1)

        def points(k):
            return jnp.broadcast_to(grid_ref[k, 0:1, :], (TILE, LANES))

        def scoped(w0, w1, s0, s1):
            weights = (w0, w1)
            scales = (s0, s1)

            def weigh(which, slot):
                a, g = which
                unit = (idx[0] + (step * per_step + a) * idx[1]) * blocks
                for jj in range(group_blocks):
                    j = g * group_blocks + jj
                    for r in range(0, rows, TILE):
                        ex = exp_ref[0, r:r + TILE, :].astype(jnp.float32)
                        ex = jnp.sum(jnp.where(lanes == unit + j, ex, 0.0), axis=1, keepdims=True)
                        ex = jnp.broadcast_to(ex, (TILE, LANES))
                        m = jj * rows + r
                        scales[slot][m:m + TILE, :] = jnp.exp2(ex) * points(NLEV)
                        cols = slice(j * LANES, (j + 1) * LANES)
                        pseudo = outer_refs[a][r:r + TILE, cols] - inner_refs[a][0, r:r + TILE, cols].astype(jnp.float32)
                        v = pseudo * (jnp.exp2(-ex) * STRETCH)
                        near = jnp.minimum(jnp.maximum(v, points(0)), points(NLEV - 1))
                        far = (v + v) - near
                        for k in range(NLEV):
                            e = (points(k) - near) * (far - points(k))
                            weights[slot][m:m + TILE, k * LANES:(k + 1) * LANES] = jnp.exp2(e).astype(jnp.bfloat16)

            def average(which, slot):
                a, g = which
                sums = jnp.dot(weights[slot][...], sum_ref[...], preferred_element_type=jnp.float32)
                coded = sums[:, LANES:] / sums[:, :LANES] * scales[slot][...]
                for jj in range(group_blocks):
                    cols = slice((g * group_blocks + jj) * LANES, (g * group_blocks + jj + 1) * LANES)
                    piece = coded[jj * rows:(jj + 1) * rows]
                    if recv_ref is not None:
                        piece = piece + recv_ref[a, :, cols].astype(jnp.float32)
                    out_ref[a, :, cols] = piece.astype(jnp.bfloat16)

            weigh(groups[0], 0)
            for n in range(1, len(groups)):
                weigh(groups[n], n % 2)
                average(groups[n - 1], (n - 1) % 2)
            average(groups[-1], (len(groups) - 1) % 2)

        pl.run_scoped(
            scoped,
            pltpu.VMEM((GROUP, NLEV * LANES), jnp.bfloat16),
            pltpu.VMEM((GROUP, NLEV * LANES), jnp.bfloat16),
            pltpu.VMEM((GROUP, LANES), jnp.float32),
            pltpu.VMEM((GROUP, LANES), jnp.float32),
        )

    def unit_of(a):
        return lambda s, idx: idx[0] + (s * per_step + a) * idx[1]

    in_specs = [
        pl.BlockSpec((NLEV + 1, 8, LANES), lambda s, idx: (0, 0, 0)),
        pl.BlockSpec((NLEV * LANES, 2 * LANES), lambda s, idx: (0, 0)),
        pl.BlockSpec((1, rows, LANES), lambda s, idx: (0, 0, 0)),
    ]
    in_specs += [pl.BlockSpec((rows, width), lambda s, idx, f=unit_of(a): (0, f(s, idx))) for a in range(per_step)]
    in_specs += [pl.BlockSpec((1, rows, width), lambda s, idx, f=unit_of(a): (0, 0, f(s, idx))) for a in range(per_step)]
    piece = pl.BlockSpec((per_step, rows, width), lambda s, idx: (s, 0, 0))
    args = [where, grid, summing, exponents] + [outer] * per_step + [inner] * per_step
    if received is not None:
        in_specs.append(piece)
        args.append(received)
    return pl.pallas_call(
        body,
        grid_spec=pltpu.PrefetchScalarGridSpec(
            num_scalar_prefetch=1, grid=(steps,), in_specs=in_specs, out_specs=piece
        ),
        out_shape=jax.ShapeDtypeStruct((owners, rows, width), jnp.bfloat16),
        cost_estimate=pl.CostEstimate(
            flops=int(owners * rows * width * 130), transcendentals=0,
            bytes_accessed=int(owners * rows * width * 8),
        ),
        name="encode_keep" if received is not None else "encode_send",
    )(*args)


def owners_mean(pieces, replicas):
    senders, rows, width = pieces.shape

    def body(in_ref, mean_ref, copies_ref, squares_ref):
        total = in_ref[0].astype(jnp.float32)
        for s in range(1, senders):
            total = total + in_ref[s].astype(jnp.float32)
        mean = total / replicas
        mean_ref[...] = mean
        half = mean.astype(jnp.bfloat16)
        for s in range(senders):
            copies_ref[s] = half
        sq = mean * mean
        acc = sq[0:8, 0:LANES]
        for r in range(0, rows, 8):
            for c in range(0, width, LANES):
                if r or c:
                    acc = acc + sq[r:r + 8, c:c + LANES]
        squares_ref[...] = acc

    return pl.pallas_call(
        body,
        out_shape=(
            jax.ShapeDtypeStruct((rows, width), jnp.float32),
            jax.ShapeDtypeStruct((senders, rows, width), jnp.bfloat16),
            jax.ShapeDtypeStruct((8, LANES), jnp.float32),
        ),
        name="owners_mean",
    )(pieces)


def blend(where, squares, entries, outer, inner, momenta, means, partial):
    rows, columns = outer.shape
    owners, _, width = momenta.shape
    spans = [m.shape[2] for m in means]

    def body(idx, sq_ref, outer_ref, inner_ref, mom_ref, *rest):
        mean_refs = rest[:len(spans)]
        out_ref = rest[-1]
        mean_square = jnp.sum(sq_ref[...]) / entries
        clip = jnp.minimum(
            1.0, clip_rms / jnp.sqrt(jnp.full((8, LANES), mean_square, jnp.float32) + 1e-06)
        )[0:1, 0:1]
        at = 0
        for span, ref in zip(spans, mean_refs):
            cols = slice(at, at + span)
            grad = clip * ref[0].astype(jnp.float32)
            momentum_next = outer_mu * mom_ref[0, :, cols].astype(jnp.float32) + grad
            outer_next = outer_ref[:, cols] - outer_rate * (grad + outer_mu * momentum_next)
            half = outer_next.astype(jnp.bfloat16).astype(jnp.float32)
            mixed = mix_rate * half + (1.0 - mix_rate) * inner_ref[0, :, cols].astype(jnp.float32)
            out_ref[0, :, cols] = mixed.astype(jnp.bfloat16)
            at += span

    def unit(d, idx):
        return idx[0] + d * idx[1]

    in_specs = [
        pl.BlockSpec((8, LANES), lambda d, idx: (0, 0)),
        pl.BlockSpec((rows, width), lambda d, idx: (0, unit(d, idx))),
        pl.BlockSpec((1, rows, width), lambda d, idx: (0, 0, unit(d, idx))),
        pl.BlockSpec((1, rows, width), lambda d, idx: (d, 0, 0)),
    ]
    in_specs += [pl.BlockSpec((1, rows, span), lambda d, idx: (d, 0, 0)) for span in spans]
    args = [where, squares, outer, inner, momenta, *means]
    aliases = {}
    if partial is not None:
        in_specs.append(pl.BlockSpec(memory_space=pl.ANY))
        aliases = {len(args): 0}
        args.append(partial)
    return pl.pallas_call(
        body,
        grid_spec=pltpu.PrefetchScalarGridSpec(
            num_scalar_prefetch=1, grid=(owners,), in_specs=in_specs,
            out_specs=pl.BlockSpec((1, rows, width), lambda d, idx: (0, 0, unit(d, idx))),
        ),
        out_shape=jax.ShapeDtypeStruct((1, rows, columns), jnp.bfloat16),
        input_output_aliases=aliases,
        name="blend",
    )(*args)


def swap(array):
    return lax.ppermute(array, CORE, [(0, 1), (1, 0)])


def exchange(array, axes):
    return lax.all_to_all(array, axes, 0, 0, tiled=False)


def per_device(replica_inner_weight, outer_weights, momentum, exponents, levels):
    replicas = lax.axis_size(REP)
    rows, columns = outer_weights.shape
    entries = rows * lax.axis_size(FSDP) * columns
    width = momentum.shape[1]
    chips = lax.axis_size(CHIPS)
    core = lax.axis_index(CORE)
    start = lax.axis_index(REP) * width

    grid, summing = prepare(levels)
    own_momenta = exchange(
        jnp.broadcast_to(momentum.astype(jnp.bfloat16)[None], (chips, rows, width)), CHIPS
    )

    starts = [sum(WIDTHS[:i]) for i in range(len(WIDTHS))]

    def place(which, at, span):
        return jnp.stack([which * (width // span) + at // span, jnp.int32(2 * (width // span))]).astype(jnp.int32)

    def code(which, i, received=None):
        return encode(
            place(which, starts[i], WIDTHS[i]), grid, summing, outer_weights, replica_inner_weight,
            exponents, WIDTHS[i], received,
        )

    received = [swap(code(1 - core, i)) for i in range(len(WIDTHS))]
    received[-1], own_momenta = lax.optimization_barrier((received[-1], own_momenta))
    means, gathered, squares = [], [], []
    for i in range(len(WIDTHS)):
        pieces = exchange(code(core, i, received[i]), CHIPS)
        mean, copies, square = owners_mean(pieces, float(replicas))
        means.append(mean)
        gathered.append(exchange(copies, CHIPS))
        squares.append(square)
    square = sum(squares[1:], squares[0])
    square = jnp.sum(exchange(jnp.broadcast_to(square[None], (8, 8, LANES)), FSDP), axis=0)
    square = jnp.sum(exchange(jnp.broadcast_to(square[None], (chips, 8, LANES)), CHIPS), axis=0)
    square = square + swap(square)
    other = [swap(g) for g in gathered]
    other_momenta = swap(own_momenta)

    unit = place(core, 0, width)
    inner_next = blend(
        unit, square, float(entries), outer_weights, replica_inner_weight, own_momenta, gathered, None
    )
    unit = place(1 - core, 0, width)
    inner_next = blend(
        unit, square, float(entries), outer_weights, replica_inner_weight, other_momenta, other, inner_next
    )
    mean_grad = jnp.concatenate(means, axis=1)
    clip = jnp.minimum(
        jnp.float32(1.0), clip_rms / jnp.sqrt(jnp.sum(square) / jnp.float32(entries) + 1e-06)
    )
    grad = clip * mean_grad
    momentum_next = outer_mu * momentum + grad
    outer_piece = lax.dynamic_slice_in_dim(outer_weights, start, width, 1)
    outer_next = outer_piece - outer_rate * (grad + outer_mu * momentum_next)
    return (inner_next, momentum_next, outer_next)


def solution(mesh):
    torus = Mesh(
        mesh.devices.reshape(4, 2, 2, 2, 4), ("rep_0", "rep_1", "rep_2", "fsdp_0", "fsdp_1")
    )
    placed = (P(REP, FSDP, None), P(FSDP, None), P(FSDP, REP), P(REP, FSDP, None), P())
    return jax.shard_map(
        per_device,
        mesh=torus,
        in_specs=placed,
        out_specs=(P(REP, FSDP, None), P(FSDP, REP), P(FSDP, REP)),
        check_vma=False,
    )
```

time: 265 us -> 180 us (0.68)
  waiting for transfers between devices: 136 us -> 46.7 us
  Pallas kernels: 0 us -> 65.7 us
  other arithmetic: 74.1 us -> 8.45 us
  starting transfers between devices: 0.08 us -> 43.3 us
  blocking collectives: 36.2 us -> 9.99 us
  between operations: 15.4 us -> 1.42 us
    reduce_scatter x1 -> x0, waiting for transfers between devices: 82.5 us -> none  [per_device(): lax.psum_scatter(coded, REP, scatter_dimension=1, tiled=True)]
    pallas_call x0 -> x9, Pallas kernels: none -> 65.7 us  [the longest x4 40 us: encode(): pl.pallas_call(body, grid_spec=pltpu.PrefetchScalarGridSpec(num_scalar_pr...]
    convert_element_type x2 -> x1, other arithmetic: 62.7 us -> 1.07 us  [per_device(): momentum.astype(jnp.bfloat16)[None]]
    all_gather x1 -> x0, waiting for transfers between devices: 53.3 us -> none  [per_device(): lax.all_gather(outer_next.astype(jnp.bfloat16), REP, axis=1, tiled=True)]
    all_to_all x0 -> x6, waiting for transfers between devices: none -> 46.5 us  [exchange(): return lax.all_to_all(array, axes, 0, 0, tiled=False)]
    psum x5 -> x0, blocking collectives: 36.2 us -> none  [by_axis(): array = lax.psum(array, axis)]
    all_to_all x0 -> x6, starting transfers between devices: none -> 30.4 us  [exchange(): return lax.all_to_all(array, axes, 0, 0, tiled=False)]
    ppermute x0 -> x6, starting transfers between devices: none -> 13 us  [swap(): return lax.ppermute(array, CORE, [(0, 1), (1, 0)])]
  transfers between devices with their start and end apart: 2 -> 12, of which waited for: 2 -> 6; matrix products, arithmetic and copies ran while one was open for 0% -> 4% of each run, Pallas kernels for 0% -> 31%
where the time goes in v1:
time: 180 us; the launch traced here: 179 us
  Pallas kernels  65.7 us (36%)
  waiting for transfers between devices  46.7 us (26%)
  starting transfers between devices  43.3 us (24%)
  blocking collectives  9.99 us (6%)
  other arithmetic  8.45 us (5%)
  local copies, waits for them, and re-layouts  3.22 us (2%)
    all_to_all x6, waiting for transfers between devices, exchange(): return lax.all_to_all(array, axes, 0, 0, tiled=False)  46.5 us
    pallas_call x4, Pallas kernels, encode(): pl.pallas_call(body, grid_spec=pltpu.PrefetchScalarGridSpec(num_scalar_pr...  40 us
    all_to_all x6, starting transfers between devices, exchange(): return lax.all_to_all(array, axes, 0, 0, tiled=False)  30.4 us
    pallas_call x2, Pallas kernels, blend(): pl.pallas_call(body, grid_spec=pltpu.PrefetchScalarGridSpec(num_scalar_pr...  18.9 us
    ppermute x6, starting transfers between devices, swap(): return lax.ppermute(array, CORE, [(0, 1), (1, 0)])  13 us
    all_to_all x1, blocking collectives, exchange(): return lax.all_to_all(array, axes, 0, 0, tiled=False)  9.99 us
    pallas_call x2, Pallas kernels, owners_mean(): pl.pallas_call(body, out_shape=(jax.ShapeDtypeStruct((rows, width), jnp.f...  5 us
  transfers between devices with their start and end apart: 12, of which 6 were waited for; matrix products, arithmetic and copies ran while one was open for 4% of the time, Pallas kernels for 31%

profile of v1, /device:TPU:1, one launch (start us, length us, event | category | flops | bytes accessed | tf_op | source)
XLA Modules:
  0.0 178.8 jit_solution(7960013790579703353)
XLA Ops:
  0.6 1.1 convert_element_type.3
  1.7 1.6 broadcast_in_dim.6
  3.3 7.5 %all-to-all-start.1 = ((bf16[8,128,1024]{2,1,0:T(8,128)(2,1)}), bf16[8,128,1024]{2,1,0:T(8,128)(2,1)S(1)}, u32[]{:S(2)}, u32[]{:S(2)}) async-start(bf16[8,128,1024]{2,1,0:T(8,128)(2,1)} %broadcast_in_dim.6), calls=%async_computation.1 | async-start | bytes 4194304 | tf_op jit(solution)/shard_map/all_to_all | solution.py:244
  10.8 1.8 prepare.1
  12.5 0.6 pad_add_fusion.2.refs_0_
  13.1 9.9 %encode_send.2 = bf16[8,128,512]{2,1,0:T(8,128)(2,1)} custom-call(s32[2]{0:T(128)} %pad_add_fusion.2.refs_0_, f32[17,8,128]{2,1,0:T(8,128)} %get-tuple-element.13.refs_1_, bf16[2048,256]{1,0:T(8,128)(2,1)} %get-tuple-element.14.refs_2_, s32[1,128,128]{2,1,0:T(8,128)} %refs_3_.7, f32[128,16384]{1,0:T(8,128)} %outer_ref.3, f32[128,16384]{1,0:T(8,128)} %outer_ref.3, ...), custom_call_target="tpu_custom_call" | custom-call | flops 68157440 | bytes 4194304 | tf_op jit(solution)/shard_map/encode_send/pallas_call | solution.py:143
  23.0 1.0 collective-permute-start
  23.9 0.7 pad_add_fusion
  24.6 9.9 %encode_send.3 = bf16[8,128,512]{2,1,0:T(8,128)(2,1)} custom-call(s32[2]{0:T(128)} %get-tuple-element.27.refs_0_, f32[17,8,128]{2,1,0:T(8,128)} %get-tuple-element.13.refs_1_, bf16[2048,256]{1,0:T(8,128)(2,1)} %get-tuple-element.14.refs_2_, s32[1,128,128]{2,1,0:T(8,128)} %refs_3_.7, f32[128,16384]{1,0:T(8,128)} %outer_ref.3, f32[128,16384]{1,0:T(8,128)} %outer_ref.3, ...), custom_call_target="tpu_custom_call" | custom-call | flops 68157440 | bytes 4194304 | tf_op jit(solution)/shard_map/encode_send/pallas_call | solution.py:143
  34.5 0.0 collective-permute-start.1
  34.5 0.6 pad_add_fusion.3.refs_0_
  35.1 0.0 collective-permute-done.refs_8_
  35.1 1.0 copy-done.3
  36.1 10.1 %encode_keep.2 = bf16[8,128,512]{2,1,0:T(8,128)(2,1)} custom-call(s32[2]{0:T(128)} %pad_add_fusion.3.refs_0_, f32[17,8,128]{2,1,0:T(8,128)} %get-tuple-element.13.refs_1_, bf16[2048,256]{1,0:T(8,128)(2,1)} %get-tuple-element.14.refs_2_, s32[1,128,128]{2,1,0:T(8,128)} %refs_3_.7, f32[128,16384]{1,0:T(8,128)} %outer_ref.3, f32[128,16384]{1,0:T(8,128)} %outer_ref.3, ...), custom_call_target="tpu_custom_call" | custom-call | flops 68157440 | bytes 4194304 | tf_op jit(solution)/shard_map/encode_keep/pallas_call | solution.py:143
  46.2 0.0 all-to-all-done.1.mom_ref
  46.2 6.9 %all-to-all-start = ((bf16[8,128,512]{2,1,0:T(8,128)(2,1)}), bf16[8,128,512]{2,1,0:T(8,128)(2,1)S(1)}, u32[]{:S(2)}, u32[]{:S(2)}) async-start(bf16[8,128,512]{2,1,0:T(8,128)(2,1)} %encode_keep.2), calls=%async_computation | async-start | bytes 2097152 | tf_op jit(solution)/shard_map/all_to_all | solution.py:244
  53.1 0.0 collective-permute-done.1.refs_8_
  53.1 10.1 %encode_keep.3 = bf16[8,128,512]{2,1,0:T(8,128)(2,1)} custom-call(s32[2]{0:T(128)} %get-tuple-element.28.refs_0_, f32[17,8,128]{2,1,0:T(8,128)} %get-tuple-element.13.refs_1_, bf16[2048,256]{1,0:T(8,128)(2,1)} %get-tuple-element.14.refs_2_, s32[1,128,128]{2,1,0:T(8,128)} %refs_3_.7, f32[128,16384]{1,0:T(8,128)} %outer_ref.3, f32[128,16384]{1,0:T(8,128)} %outer_ref.3, ...), custom_call_target="tpu_custom_call" | custom-call | flops 68157440 | bytes 4194304 | tf_op jit(solution)/shard_map/encode_keep/pallas_call | solution.py:143
  63.3 6.4 %all-to-all-done.in_ref = bf16[8,128,512]{2,1,0:T(8,128)(2,1)S(1)} async-done(((bf16[8,128,512]{2,1,0:T(8,128)(2,1)}), bf16[8,128,512]{2,1,0:T(8,128)(2,1)S(1)}, u32[]{:S(2)}, u32[]{:S(2)}) %all-to-all-start) | async-done | bytes 1048608 | tf_op jit(solution)/shard_map/all_to_all | solution.py:244
  69.6 4.2 %all-to-all-start.2 = ((bf16[8,128,512]{2,1,0:T(8,128)(2,1)}), bf16[8,128,512]{2,1,0:T(8,128)(2,1)}, u32[]{:S(2)}, u32[]{:S(2)}) async-start(bf16[8,128,512]{2,1,0:T(8,128)(2,1)} %encode_keep.3), calls=%async_computation.2 | async-start | bytes 2097152 | tf_op jit(solution)/shard_map/all_to_all | solution.py:244
  73.9 0.0 copy-done.2
  73.9 2.6 %owners_mean.2 = (f32[128,512]{1,0:T(8,128)}, bf16[8,128,512]{2,1,0:T(8,128)(2,1)}, f32[8,128]{1,0:T(8,128)}) custom-call(bf16[8,128,512]{2,1,0:T(8,128)(2,1)} %copy-done.2), custom_call_target="tpu_custom_call" | custom-call | tf_op jit(solution)/shard_map/owners_mean/pallas_call | solution.py:177
  76.5 12.8 %all-to-all-done.2.in_ref = bf16[8,128,512]{2,1,0:T(8,128)(2,1)} async-done(((bf16[8,128,512]{2,1,0:T(8,128)(2,1)}), bf16[8,128,512]{2,1,0:T(8,128)(2,1)}, u32[]{:S(2)}, u32[]{:S(2)}) %all-to-all-start.2) | async-done | bytes 1048608 | tf_op jit(solution)/shard_map/all_to_all | solution.py:244
  89.2 4.1 %all-to-all-start.5 = ((bf16[8,128,512]{2,1,0:T(8,128)(2,1)}), bf16[8,128,512]{2,1,0:T(8,128)(2,1)S(1)}, u32[]{:S(2)}, u32[]{:S(2)}) async-start(bf16[8,128,512]{2,1,0:T(8,128)(2,1)} %get-tuple-element.19), calls=%async_computation.5 | async-start | bytes 2097152 | tf_op jit(solution)/shard_map/all_to_all | solution.py:244
  93.4 0.0 copy-done
  93.4 2.4 %collective-permute-start.3 = (bf16[8,128,1024]{2,1,0:T(8,128)(2,1)S(1)}, bf16[8,128,1024]{2,1,0:T(8,128)(2,1)}, u32[]{:S(2)}, u32[]{:S(2)}) collective-permute-start(bf16[8,128,1024]{2,1,0:T(8,128)(2,1)S(1)} %all-to-all-done.1.mom_ref), channel_id=1, source_target_pairs={{0,8},{8,0},{1,9},{9,1},{2,10},{10,2},{3,11},{11,3},{4,12},{12,4},... | collective-permute-start | bytes 6291464 | tf_op jit(solution)/shard_map/ppermute | solution.py:240
  95.7 2.4 %owners_mean.3 = (f32[128,512]{1,0:T(8,128)}, bf16[8,128,512]{2,1,0:T(8,128)(2,1)}, f32[8,128]{1,0:T(8,128)}) custom-call(bf16[8,128,512]{2,1,0:T(8,128)(2,1)} %all-to-all-done.2.in_ref), custom_call_target="tpu_custom_call" | custom-call | tf_op jit(solution)/shard_map/owners_mean/pallas_call | solution.py:177
  98.2 10.3 %all-to-all-done.5.rest_0_ = bf16[8,128,512]{2,1,0:T(8,128)(2,1)S(1)} async-done(((bf16[8,128,512]{2,1,0:T(8,128)(2,1)}), bf16[8,128,512]{2,1,0:T(8,128)(2,1)S(1)}, u32[]{:S(2)}, u32[]{:S(2)}) %all-to-all-start.5) | async-done | bytes 1048608 | tf_op jit(solution)/shard_map/all_to_all | solution.py:244
  108.4 4.2 %all-to-all-start.6 = ((bf16[8,128,512]{2,1,0:T(8,128)(2,1)}), bf16[8,128,512]{2,1,0:T(8,128)(2,1)}, u32[]{:S(2)}, u32[]{:S(2)}) async-start(bf16[8,128,512]{2,1,0:T(8,128)(2,1)} %get-tuple-element.20), calls=%async_computation.6 | async-start | bytes 2097152 | tf_op jit(solution)/shard_map/all_to_all | solution.py:244
  112.7 3.1 %collective-permute-start.4 = (bf16[8,128,512]{2,1,0:T(8,128)(2,1)S(1)}, bf16[8,128,512]{2,1,0:T(8,128)(2,1)}, u32[]{:S(2)}, u32[]{:S(2)}) collective-permute-start(bf16[8,128,512]{2,1,0:T(8,128)(2,1)S(1)} %all-to-all-done.5.rest_0_), channel_id=1, source_target_pairs={{0,8},{8,0},{1,9},{9,1},{2,10},{10,2},{3,11},{11,3},{4,12},{12,4},... | collective-permute-start | bytes 3145736 | tf_op jit(solution)/shard_map/ppermute | solution.py:240
  115.8 11.1 %all-to-all-done.6.rest_1_ = bf16[8,128,512]{2,1,0:T(8,128)(2,1)} async-done(((bf16[8,128,512]{2,1,0:T(8,128)(2,1)}), bf16[8,128,512]{2,1,0:T(8,128)(2,1)}, u32[]{:S(2)}, u32[]{:S(2)}) %all-to-all-start.6) | async-done | bytes 1048608 | tf_op jit(solution)/shard_map/all_to_all | solution.py:244
  126.9 3.9 %collective-permute-start.5 = (bf16[8,128,512]{2,1,0:T(8,128)(2,1)}, bf16[8,128,512]{2,1,0:T(8,128)(2,1)}, u32[]{:S(2)}, u32[]{:S(2)}) collective-permute-start(bf16[8,128,512]{2,1,0:T(8,128)(2,1)} %all-to-all-done.6.rest_1_), channel_id=1, source_target_pairs={{0,8},{8,0},{1,9},{9,1},{2,10},{10,2},{3,11},{11,3},{4,12},{12,4},... | collective-permute-start | bytes 3145736 | tf_op jit(solution)/shard_map/ppermute | solution.py:240
  130.9 0.7 add.32
  131.6 10.0 %all_to_all.35 = f32[8,8,128]{2,1,0:T(8,128)S(1)} all-to-all(f32[8,8,128]{2,1,0:T(8,128)S(1)} %broadcast_in_dim.7), channel_id=1, replica_groups=mesh['rep_0'=4,'rep_1'=2,'rep_2'=2,'fsdp_0'=2,'fsdp_1'=4] {'fsdp_0','fsd..., dimensions={0} | all-to-all | bytes 65536 | tf_op jit(solution)/shard_map/all_to_all | solution.py:244
  141.6 0.6 broadcast_in_dim.8
  142.2 3.3 %all-to-all-start.4 = ((f32[8,8,128]{2,1,0:T(8,128)}), f32[8,8,128]{2,1,0:T(8,128)S(1)}, u32[]{:S(2)}, u32[]{:S(2)}) async-start(f32[8,8,128]{2,1,0:T(8,128)} %broadcast_in_dim.8), calls=%async_computation.4 | async-start | bytes 65536 | tf_op jit(solution)/shard_map/all_to_all | solution.py:244
  145.5 0.6 pad_add_fusion.5.idx
  146.1 6.0 %all-to-all-done.4 = f32[8,8,128]{2,1,0:T(8,128)S(1)} async-done(((f32[8,8,128]{2,1,0:T(8,128)}), f32[8,8,128]{2,1,0:T(8,128)S(1)}, u32[]{:S(2)}, u32[]{:S(2)}) %all-to-all-start.4) | async-done | bytes 32800 | tf_op jit(solution)/shard_map/all_to_all | solution.py:244
  152.1 2.6 %collective-permute-start.2 = (f32[8,128]{1,0:T(8,128)S(1)}, f32[8,128]{1,0:T(8,128)S(1)}, u32[]{:S(2)}, u32[]{:S(2)}) collective-permute-start(f32[8,128]{1,0:T(8,128)S(1)} %reduce_sum.28), channel_id=1, source_target_pairs={{0,8},{8,0},{1,9},{9,1},{2,10},{10,2},{3,11},{11,3},{4,12},{12,4},... | collective-permute-start | bytes 12296 | tf_op jit(solution)/shard_map/ppermute | solution.py:240
  154.7 0.6 pad_add_fusion.4.idx
  155.3 0.2 collective-permute-done.2
  155.5 1.2 fusion
  157.4 2.5 %multiply_subtract_fusion = (f32[128,1024]{1,0:T(8,128)}, f32[128,1024]{1,0:T(8,128)}) fusion(f32[128,16384]{1,0:T(8,128)} %outer_ref.3, s32[]{:T(128)S(6)} %select_n.3, f32[128,512]{1,0:T(8,128)} %get-tuple-element.22, f32[128,512]{1,0:T(8,128)S(1)} %copy-done.4, f32[]{:T(128)S(6)} %min_shard_map.3, f32[128,1024]{1,0:T(8,128)} %param.7), kind=kLoop, calls=%fused_computation.1 | loop fusion | flops 1048576 | bytes 2621448 | tf_op jit(solution)/shard_map/sub | solution.py:303
  159.9 9.5 %blend.2.rest_2_ = bf16[1,128,16384]{2,1,0:T(8,128)(2,1)} custom-call(s32[2]{0:T(128)} %pad_add_fusion.4.idx, f32[8,128]{1,0:T(8,128)} %get-tuple-element.26.sq_ref, f32[128,16384]{1,0:T(8,128)} %outer_ref.3, bf16[1,128,16384]{2,1,0:T(8,128)(2,1)} %inner_ref.3, bf16[8,128,1024]{2,1,0:T(8,128)(2,1)} %copy-done, bf16[8,128,512]{2,1,0:T(8,128)(2,1)} %copy-done.1, ...), custom_call_target="tpu_custom_call" | custom-call | tf_op jit(solution)/shard_map/blend/pallas_call | solution.py:227
  169.3 0.0 collective-permute-done.3.mom_ref
  169.3 0.0 collective-permute-done.4.rest_0_
  169.3 0.0 collective-permute-done.5.rest_1_
  169.3 9.5 %blend.3 = bf16[1,128,16384]{2,1,0:T(8,128)(2,1)} custom-call(s32[2]{0:T(128)} %pad_add_fusion.5.idx, f32[8,128]{1,0:T(8,128)} %get-tuple-element.26.sq_ref, f32[128,16384]{1,0:T(8,128)} %outer_ref.3, bf16[1,128,16384]{2,1,0:T(8,128)(2,1)} %inner_ref.3, bf16[8,128,1024]{2,1,0:T(8,128)(2,1)} %collective-permute-done.3.mom_ref, ...), custom_call_target="tpu_custom_call", output_to_operand_aliasing={{}: (7, {})} | custom-call | tf_op jit(solution)/shard_map/blend/pallas_call | solution.py:227
  (12 shorter events, 0.0 us)
Async XLA Ops:
  3.3 42.9 %all-to-all-start.1 = ((bf16[8,128,1024]{2,1,0:T(8,128)(2,1)}), bf16[8,128,1024]{2,1,0:T(8,128)(2,1)S(1)}, u32[]{:S(2)}, u32[]{:S(2)}) async-start(bf16[8,128,1024]{2,1,0:T(8,128)(2,1)} %broadcast_in_dim.6), calls=%async_computation.1 | async-start | bytes 4194304 | tf_op jit(solution)/shard_map/all_to_all | solution.py:244
  23.0 12.1 %collective-permute-start = (bf16[8,128,512]{2,1,0:T(8,128)(2,1)}, bf16[8,128,512]{2,1,0:T(8,128)(2,1)S(1)}, u32[]{:S(2)}, u32[]{:S(2)}) collective-permute-start(bf16[8,128,512]{2,1,0:T(8,128)(2,1)} %encode_send.2), channel_id=1, source_target_pairs={{0,8},{8,0},{1,9},{9,1},{2,10},{10,2},{3,11},{11,3},{4,12},{12,4},... | collective-permute-start | bytes 3145736 | tf_op jit(solution)/shard_map/ppermute | solution.py:240
  34.5 18.7 %collective-permute-start.1 = (bf16[8,128,512]{2,1,0:T(8,128)(2,1)}, bf16[8,128,512]{2,1,0:T(8,128)(2,1)}, u32[]{:S(2)}, u32[]{:S(2)}) collective-permute-start(bf16[8,128,512]{2,1,0:T(8,128)(2,1)} %encode_send.3), channel_id=1, source_target_pairs={{0,8},{8,0},{1,9},{9,1},{2,10},{10,2},{3,11},{11,3},{4,12},{12,4},... | collective-permute-start | bytes 3145736 | tf_op jit(solution)/shard_map/ppermute | solution.py:240
  35.1 1.0 copy-start.3
  46.2 47.2 %copy-start = (bf16[8,128,1024]{2,1,0:T(8,128)(2,1)}, bf16[8,128,1024]{2,1,0:T(8,128)(2,1)S(1)}, u32[]{:S(2)}) copy-start(bf16[8,128,1024]{2,1,0:T(8,128)(2,1)S(1)} %all-to-all-done.1.mom_ref) | copy-start | bytes 6291460
  46.2 23.5 %all-to-all-start = ((bf16[8,128,512]{2,1,0:T(8,128)(2,1)}), bf16[8,128,512]{2,1,0:T(8,128)(2,1)S(1)}, u32[]{:S(2)}, u32[]{:S(2)}) async-start(bf16[8,128,512]{2,1,0:T(8,128)(2,1)} %encode_keep.2), calls=%async_computation | async-start | bytes 2097152 | tf_op jit(solution)/shard_map/all_to_all | solution.py:244
  69.6 4.3 %copy-start.2 = (bf16[8,128,512]{2,1,0:T(8,128)(2,1)}, bf16[8,128,512]{2,1,0:T(8,128)(2,1)S(1)}, u32[]{:S(2)}) copy-start(bf16[8,128,512]{2,1,0:T(8,128)(2,1)S(1)} %all-to-all-done.in_ref) | copy-start | bytes 3145732
  69.6 19.6 %all-to-all-start.2 = ((bf16[8,128,512]{2,1,0:T(8,128)(2,1)}), bf16[8,128,512]{2,1,0:T(8,128)(2,1)}, u32[]{:S(2)}, u32[]{:S(2)}) async-start(bf16[8,128,512]{2,1,0:T(8,128)(2,1)} %encode_keep.3), calls=%async_computation.2 | async-start | bytes 2097152 | tf_op jit(solution)/shard_map/all_to_all | solution.py:244
  76.5 54.4 %copy-start.5 = (f32[8,128]{1,0:T(8,128)S(1)}, f32[8,128]{1,0:T(8,128)}, u32[]{:S(2)}) copy-start(f32[8,128]{1,0:T(8,128)} %get-tuple-element.15) | copy-start | bytes 12292
  76.5 80.9 %copy-start.4 = (f32[128,512]{1,0:T(8,128)S(1)}, f32[128,512]{1,0:T(8,128)}, u32[]{:S(2)}) copy-start(f32[128,512]{1,0:T(8,128)} %get-tuple-element.21) | copy-start | bytes 786436
  89.2 19.2 %all-to-all-start.5 = ((bf16[8,128,512]{2,1,0:T(8,128)(2,1)}), bf16[8,128,512]{2,1,0:T(8,128)(2,1)S(1)}, u32[]{:S(2)}, u32[]{:S(2)}) async-start(bf16[8,128,512]{2,1,0:T(8,128)(2,1)} %get-tuple-element.19), calls=%async_computation.5 | async-start | bytes 2097152 | tf_op jit(solution)/shard_map/all_to_all | solution.py:244
  93.4 76.0 %collective-permute-start.3 = (bf16[8,128,1024]{2,1,0:T(8,128)(2,1)S(1)}, bf16[8,128,1024]{2,1,0:T(8,128)(2,1)}, u32[]{:S(2)}, u32[]{:S(2)}) collective-permute-start(bf16[8,128,1024]{2,1,0:T(8,128)(2,1)S(1)} %all-to-all-done.1.mom_ref), channel_id=1, source_target_pairs={{0,8},{8,0},{1,9},{9,1},{2,10},{10,2},{3,11},{11,3},{4,12},{12,4},... | collective-permute-start | bytes 6291464 | tf_op jit(solution)/shard_map/ppermute | solution.py:240
  108.4 51.4 %copy-start.1 = (bf16[8,128,512]{2,1,0:T(8,128)(2,1)}, bf16[8,128,512]{2,1,0:T(8,128)(2,1)S(1)}, u32[]{:S(2)}) copy-start(bf16[8,128,512]{2,1,0:T(8,128)(2,1)S(1)} %all-to-all-done.5.rest_0_) | copy-start | bytes 3145732
  108.4 18.5 %all-to-all-start.6 = ((bf16[8,128,512]{2,1,0:T(8,128)(2,1)}), bf16[8,128,512]{2,1,0:T(8,128)(2,1)}, u32[]{:S(2)}, u32[]{:S(2)}) async-start(bf16[8,128,512]{2,1,0:T(8,128)(2,1)} %get-tuple-element.20), calls=%async_computation.6 | async-start | bytes 2097152 | tf_op jit(solution)/shard_map/all_to_all | solution.py:244
  112.7 56.6 %collective-permute-start.4 = (bf16[8,128,512]{2,1,0:T(8,128)(2,1)S(1)}, bf16[8,128,512]{2,1,0:T(8,128)(2,1)}, u32[]{:S(2)}, u32[]{:S(2)}) collective-permute-start(bf16[8,128,512]{2,1,0:T(8,128)(2,1)S(1)} %all-to-all-done.5.rest_0_), channel_id=1, source_target_pairs={{0,8},{8,0},{1,9},{9,1},{2,10},{10,2},{3,11},{11,3},{4,12},{12,4},... | collective-permute-start | bytes 3145736 | tf_op jit(solution)/shard_map/ppermute | solution.py:240
  126.9 42.4 %collective-permute-start.5 = (bf16[8,128,512]{2,1,0:T(8,128)(2,1)}, bf16[8,128,512]{2,1,0:T(8,128)(2,1)}, u32[]{:S(2)}, u32[]{:S(2)}) collective-permute-start(bf16[8,128,512]{2,1,0:T(8,128)(2,1)} %all-to-all-done.6.rest_1_), channel_id=1, source_target_pairs={{0,8},{8,0},{1,9},{9,1},{2,10},{10,2},{3,11},{11,3},{4,12},{12,4},... | collective-permute-start | bytes 3145736 | tf_op jit(solution)/shard_map/ppermute | solution.py:240
  142.2 9.9 %all-to-all-start.4 = ((f32[8,8,128]{2,1,0:T(8,128)}), f32[8,8,128]{2,1,0:T(8,128)S(1)}, u32[]{:S(2)}, u32[]{:S(2)}) async-start(f32[8,8,128]{2,1,0:T(8,128)} %broadcast_in_dim.8), calls=%async_computation.4 | async-start | bytes 65536 | tf_op jit(solution)/shard_map/all_to_all | solution.py:244
  152.1 3.4 %collective-permute-start.2 = (f32[8,128]{1,0:T(8,128)S(1)}, f32[8,128]{1,0:T(8,128)S(1)}, u32[]{:S(2)}, u32[]{:S(2)}) collective-permute-start(f32[8,128]{1,0:T(8,128)S(1)} %reduce_sum.28), channel_id=1, source_target_pairs={{0,8},{8,0},{1,9},{9,1},{2,10},{10,2},{3,11},{11,3},{4,12},{12,4},... | collective-permute-start | bytes 12296 | tf_op jit(solution)/shard_map/ppermute | solution.py:240
